TPU v7x, 32 devices: a whole 2x2x4 slice. The times are simulated.
32 devices in a mesh: dp: 4 (over y, core), row: 2 (over x), col: 4 (over z).
Axes of the slice: x: 2, y: 2, z: 4, core: 2. Of those that a mesh axis runs over, the one named last changes fastest.
Arguments:
- images: bfloat16 [4, 64, 32, 1024], P('dp', None, 'row', 'col'), may hold values from -6 to 6
- first_kernel: bfloat16 [64, 64, 3, 3], replicated, may hold values from -0.25 to 0.25
- second_kernel: bfloat16 [64, 64, 3, 3], replicated, may hold values from -0.25 to 0.25
- cotangent: bfloat16 [4, 64, 32, 1024], P('dp', None, 'row', 'col'), may hold values from -6 to 6
Outputs:
- outputs: bfloat16 [4, 64, 32, 1024], P('dp', None, 'row', 'col')
- input_grad: bfloat16 [4, 64, 32, 1024], P('dp', None, 'row', 'col')
- first_grad: float32 [64, 64, 3, 3], replicated
- second_grad: float32 [64, 64, 3, 3], replicated
All inputs are finite; a program needn't handle non-finite values.
Results may differ from a plain program's by a relative error of at most 0.005.
Values may be sent and summed in bfloat16 or wider, within the bound.
No kernel may reach another device: no remote copies, remote signals or barrier semaphores. Data moves between devices by JAX's collectives and lax.ppermute only.
A program may use at most 64 MiB of HBM per device.

v0:
```python
import math
import jax
import jax.numpy as jnp
from jax import lax
from jax.sharding import PartitionSpec as P


def extended(array, sides, width):
    for axis, dim in sides:
        size, length = (lax.axis_size(axis), array.shape[dim])
        up = [(i, (i + 1) % size) for i in range(size - 1)]
        down = [(j, i) for i, j in up]
        last = lax.slice_in_dim(array, length - width, length, axis=dim)
        leading = lax.slice_in_dim(array, 0, width, axis=dim)
        before = lax.ppermute(last, axis, up)
        after = lax.ppermute(leading, axis, down)
        array = jnp.concatenate([before, array, after], axis=dim)
    return array


def convolve(padded, kernel):
    return lax.conv_general_dilated(
        padded,
        kernel,
        (1, 1),
        "VALID",
        dimension_numbers=("NCHW", "OIHW", "NCHW"),
        preferred_element_type=jnp.float32,
    )


def flipped(kernel):
    return jnp.flip(kernel, (2, 3)).transpose(1, 0, 2, 3)


def silu_grad(value):
    sigma = jax.nn.sigmoid(value)
    return sigma * (1.0 + value * (1.0 - sigma))


def kernel_grad(padded, upstream):
    height = upstream.shape[2]
    breadth = upstream.shape[3]
    outer = []
    for offset_row in range(3):
        inner = []
        for offset_col in range(3):
            window = padded[
                :, :, offset_row : offset_row + height, offset_col : offset_col + breadth
            ]
            inner.append(
                jnp.einsum("nihw,nohw->oi", window, upstream, preferred_element_type=jnp.float32)
            )
        outer.append(jnp.stack(inner, -1))
    return jnp.stack(outer, 2)


def grid_mask(height, breadth):
    row_index = lax.axis_index("row") * height + jnp.arange(height + 2, dtype=jnp.int32) - 1
    col_index = lax.axis_index("col") * breadth + jnp.arange(breadth + 2, dtype=jnp.int32) - 1
    row_valid = (row_index >= 0) & (row_index < height * lax.axis_size("row"))
    col_valid = (col_index >= 0) & (col_index < breadth * lax.axis_size("col"))
    return (row_valid[:, None] & col_valid[None, :]).astype(jnp.float32)


def on_device(images, first_kernel, second_kernel, cotangent):
    channels = images.shape[1]
    height = images.shape[2]
    breadth = images.shape[3]
    total_pixels = (
        images.shape[0]
        * height
        * breadth
        * lax.axis_size("dp")
        * lax.axis_size("row")
        * lax.axis_size("col")
    )
    factor = 1.0 / math.sqrt(total_pixels)
    stacked = jnp.concatenate((images, cotangent), axis=1)
    both = extended(stacked, (("row", 2), ("col", 3)), 2)
    widened = both[:, :channels]
    widened_cot = both[:, channels:]
    inside = grid_mask(height, breadth)
    hidden = convolve(widened, first_kernel)
    act_padded = (jax.nn.silu(hidden) * inside).astype(jnp.bfloat16)
    padded_in = widened[:, :, 1:-1, 1:-1]
    outputs = convolve(act_padded, second_kernel).astype(jnp.bfloat16)
    second_grad = kernel_grad(act_padded, cotangent)
    act_grad = convolve(widened_cot, flipped(second_kernel))
    hid_padded = (act_grad * silu_grad(hidden) * inside).astype(jnp.bfloat16)
    hid_grad = hid_padded[:, :, 1:-1, 1:-1]
    input_grad = convolve(hid_padded, flipped(first_kernel)).astype(jnp.bfloat16)
    first_grad = kernel_grad(padded_in, hid_grad)
    first_grad, second_grad = lax.psum((first_grad, second_grad), ("dp", "row", "col"))
    return (outputs, input_grad, first_grad * factor, second_grad * factor)


def solution(mesh):
    in_specs = (P("dp", None, "row", "col"), P(), P(), P("dp", None, "row", "col"))
    out_specs = (P("dp", None, "row", "col"), P("dp", None, "row", "col"), P(), P())
    return jax.shard_map(
        on_device, mesh=mesh, in_specs=in_specs, out_specs=out_specs, check_vma=False
    )
```

profile of v0, /device:TPU:0, one launch (start us, length us, event | category | flops | bytes accessed | tf_op | source)
XLA Modules:
  0.0 264.4 jit_solution(4958273212836746187)
XLA Ops:
  7.2 1.2 copy_dynamic-update-slice_fusion.1
  8.5 1.2 copy_dynamic-update-slice_fusion
  9.7 4.9 %collective-permute-start = (bf16[1,128,2,256]{3,1,2,0:T(8,128)(2,1)S(1)}, bf16[1,128,2,256]{3,1,2,0:T(8,128)(2,1)S(1)}, u32[]{:S(2)}, u32[]{:S(2)}) collective-permute-start(bf16[1,128,2,256]{3,1,2,0:T(8,128)(2,1)S(1)} %get-tuple-element.22), channel_id=1, source_target_pairs={{0,4},{1,5},{2,6},{3,7},{8,12},{9,13},{10,14},{11,15},{16,20},{17,... | collective-permute-start | bytes 393224 | tf_op jit(solution)/shard_map/ppermute | solution.py:15
  14.6 1.3 collective-permute-start.1
  15.9 1.4 collective-permute-done
  17.3 4.1 %collective-permute-done.1 = bf16[1,128,2,256]{3,1,2,0:T(8,128)(2,1)S(1)} collective-permute-done((bf16[1,128,2,256]{3,1,2,0:T(8,128)(2,1)S(1)}, bf16[1,128,2,256]{3,1,2,0:T(8,128)(2,1)S(1)}, u32[]{:S(2)}, u32[]{:S(2)}) %collective-permute-start.1) | collective-permute-done | bytes 131104 | tf_op jit(solution)/shard_map/ppermute | solution.py:16
  22.2 3.5 %collective-permute-start.2 = (bf16[1,128,20,2]{1,3,2,0:T(2,128)(2,1)S(1)}, bf16[1,128,20,2]{1,3,2,0:T(2,128)(2,1)S(1)}, u32[]{:S(2)}, u32[]{:S(2)}) collective-permute-start(bf16[1,128,20,2]{1,3,2,0:T(2,128)(2,1)S(1)} %copy.72), channel_id=1, source_target_pairs={{0,1},{1,2},{2,3},{4,5},{5,6},{6,7},{8,9},{9,10},{10,11},{12,13},{... | collective-permute-start | bytes 30728 | tf_op jit(solution)/shard_map/ppermute | solution.py:15
  26.0 1.3 collective-permute-start.3
  27.8 3.8 %collective-permute-done.3 = bf16[1,128,20,2]{1,3,2,0:T(2,128)(2,1)S(1)} collective-permute-done((bf16[1,128,20,2]{1,3,2,0:T(2,128)(2,1)S(1)}, bf16[1,128,20,2]{1,3,2,0:T(2,128)(2,1)S(1)}, u32[]{:S(2)}, u32[]{:S(2)}) %collective-permute-start.3) | collective-permute-done | bytes 10272 | tf_op jit(solution)/shard_map/ppermute | solution.py:16
  32.9 1.2 pad_maximum_fusion
  34.4 3.5 %reshape.214 = bf16[64,20,1,8,33]{4,3,0,1,2:T(8,128)(2,1)} reshape(bf16[64,20,1,264]{3,0,1,2:T(8,128)(2,1)S(1)} %pad) | data formatting | bytes 1351680 | tf_op jit(solution)/shard_map/conv_general_dilated | solution.py:22
  37.9 4.6 %copy.78 = bf16[64,20,1,8,33]{0,3,4,1,2:T(8,128)(2,1)} copy(bf16[64,20,1,8,33]{4,3,0,1,2:T(8,128)(2,1)} %reshape.214) | data formatting | bytes 1351680 | tf_op jit(solution)/shard_map/conv_general_dilated | solution.py:22
  42.5 0.9 slice.133
  43.6 3.3 %reshape.216 = bf16[64,20,1,8,33]{4,3,0,1,2:T(8,128)(2,1)} reshape(bf16[64,20,1,264]{3,0,1,2:T(8,128)(2,1)S(1)} %pad.4) | data formatting | bytes 1351680 | tf_op jit(solution)/shard_map/conv_general_dilated | solution.py:22
  46.9 4.7 %copy.87 = bf16[64,20,1,8,33]{0,3,4,1,2:T(8,128)(2,1)} copy(bf16[64,20,1,8,33]{4,3,0,1,2:T(8,128)(2,1)} %reshape.216) | data formatting | bytes 1351680 | tf_op jit(solution)/shard_map/conv_general_dilated | solution.py:22
  51.6 0.9 slice.138
  52.5 4.5 %fusion.4 = (f32[18,8,33,64]{3,1,2,0:T(8,128)}, f32[18,8,33,64]{3,1,2,0:T(8,128)S(1)}) fusion(pred[8,33]{0,1:T(8,128)(4,1)S(1)} %copy-done.25, bf16[64,64,3,3]{1,0,3,2:T(8,128)(2,1)S(1)} %copy-done, bf16[64,20,1,7,2]{0,3,4,1,2:T(8,128)(2,1)S(1)} %slice.133, bf16[64,20,1,8,33]{0,3,4,1,2:T(8,128)(2,1)S(1)} %copy-done.7), kind=kOutput, calls=%fused_computation.8 | convolution fusion | flops 354026496 | bytes 3218696 | tf_op jit(solution)/shard_map/conv_general_dilated | solution.py:22
  57.0 3.7 %select_multiply_fusion = f32[18,8,33,64]{3,1,2,0:T(8,128)} fusion(f32[18,8,33,64]{3,1,2,0:T(8,128)S(1)} %get-tuple-element.27, bf16[64,64,3,3]{1,0,3,2:T(8,128)(2,1)S(1)} %copy-done.24, bf16[64,20,1,7,2]{0,3,4,1,2:T(8,128)(2,1)S(1)} %slice.138, bf16[64,20,1,8,33]{0,3,4,1,2:T(8,128)(2,1)S(1)} %copy-done.8, pred[8,33]{0,1:T(8,128)(4,1)S(1)} %copy-done.25), kind=kOutput, calls=%fused_computation.6 | convolution fusion | flops 355547136 | bytes 3218696 | tf_op jit(solution)/shard_map/conv_general_dilated | solution.py:22
  60.8 5.2 %copy.127 = f32[18,8,33,64]{2,1,3,0:T(8,128)} copy(f32[18,8,33,64]{3,1,2,0:T(8,128)} %select_multiply_fusion) | data formatting | bytes 2433024 | tf_op jit(solution)/shard_map/mul | solution.py:90
  65.9 3.9 %reshape.213 = f32[18,1,264,64]{2,3,0,1:T(8,128)S(1)} reshape(f32[18,8,33,64]{2,1,3,0:T(8,128)} %copy.127) | data formatting | bytes 2433024 | tf_op jit(solution)/shard_map/mul | solution.py:90
  69.8 5.1 %copy.126 = f32[18,8,33,64]{2,1,3,0:T(8,128)} copy(f32[18,8,33,64]{3,1,2,0:T(8,128)} %get-tuple-element.26) | data formatting | bytes 2433024 | tf_op jit(solution)/shard_map/jit(silu)/mul | solution.py:85
  74.9 5.0 %reshape.212 = f32[18,1,264,64]{2,3,0,1:T(8,128)} reshape(f32[18,8,33,64]{2,1,3,0:T(8,128)} %copy.126) | data formatting | bytes 2433024 | tf_op jit(solution)/shard_map/jit(silu)/mul | solution.py:85
  79.9 3.4 %fusion.83 = (bf16[1,64,18,258]{3,1,2,0:T(8,128)(2,1)S(1)}, bf16[64,18,1,258]{3,0,1,2:T(8,128)(2,1)}, bf16[64,18,1,258]{3,0,1,2:T(8,128)(2,1)S(1)}, bf16[1,64,18,258]{3,1,2,0:T(8,128)(2,1)}) fusion(f32[18,258]{1,0:T(8,128)S(1)} %and_convert_fusion, f32[18,1,264,64]{2,3,0,1:T(8,128)} %reshape.212, f32[18,1,264,64]{2,3,0,1:T(8,128)S(1)} %reshape.213), kind=kLoop, calls=%fused_computation.124 | loop fusion | flops 1188864 | bytes 4774032 | tf_op jit(solution)/shard_map/convert_element_type | solution.py:85
  83.3 1.0 convolution_bitcast_fusion.3
  84.4 1.0 convolution_bitcast_fusion.4
  85.4 0.9 convolution_bitcast_fusion.5
  86.3 1.0 convolution_bitcast_fusion.6
  87.4 1.0 convolution_bitcast_fusion.7
  88.4 0.9 convolution_bitcast_fusion.8
  89.3 1.0 convolution_bitcast_fusion
  90.4 1.0 convolution_bitcast_fusion.1
  91.4 0.9 convolution_bitcast_fusion.2
  92.3 1.1 pad.6
  93.4 3.5 %reshape.217 = bf16[64,18,1,8,33]{4,3,0,1,2:T(8,128)(2,1)S(1)} reshape(bf16[64,18,1,264]{3,0,1,2:T(8,128)(2,1)} %pad.6) | data formatting | bytes 1216512 | tf_op jit(solution)/shard_map/conv_general_dilated | solution.py:22
  96.9 2.7 %copy.92 = bf16[64,18,1,8,33]{0,3,4,1,2:T(8,128)(2,1)} copy(bf16[64,18,1,8,33]{4,3,0,1,2:T(8,128)(2,1)S(1)} %reshape.217) | data formatting | bytes 1216512 | tf_op jit(solution)/shard_map/conv_general_dilated | solution.py:22
  99.6 0.9 slice.140
  100.5 2.9 %select_convert_fusion = bf16[16,8,33,64]{3,1,2,0:T(8,128)(2,1)S(1)} fusion(bf16[64,64,3,3]{1,0,3,2:T(8,128)(2,1)S(1)} %copy-done, bf16[64,18,1,7,2]{0,3,4,1,2:T(8,128)(2,1)S(1)} %slice.140, bf16[64,18,1,8,33]{0,3,4,1,2:T(8,128)(2,1)} %copy.92, pred[8,33]{0,1:T(8,128)(4,1)} %constant.49), kind=kOutput, calls=%fused_computation.9 | convolution fusion | flops 313903104 | bytes 1255176 | tf_op jit(solution)/shard_map/conv_general_dilated | solution.py:22
  103.8 2.2 copy.116
  106.0 1.0 pad.2
  107.0 3.5 %reshape.215 = bf16[64,18,1,8,33]{4,3,0,1,2:T(8,128)(2,1)S(1)} reshape(bf16[64,18,1,264]{3,0,1,2:T(8,128)(2,1)} %pad.2) | data formatting | bytes 1216512 | tf_op jit(solution)/shard_map/conv_general_dilated | solution.py:22
  110.5 2.7 %copy.83 = bf16[64,18,1,8,33]{0,3,4,1,2:T(8,128)(2,1)} copy(bf16[64,18,1,8,33]{4,3,0,1,2:T(8,128)(2,1)S(1)} %reshape.215) | data formatting | bytes 1216512 | tf_op jit(solution)/shard_map/conv_general_dilated | solution.py:22
  113.2 0.9 slice.135
  114.1 4.0 %select_convert_fusion.1 = bf16[16,8,33,64]{3,1,2,0:T(8,128)(2,1)S(1)} fusion(bf16[64,64,3,3]{1,0,3,2:T(8,128)(2,1)} %param.6, bf16[64,18,1,7,2]{0,3,4,1,2:T(8,128)(2,1)S(1)} %slice.135, bf16[64,18,1,8,33]{0,3,4,1,2:T(8,128)(2,1)} %copy.83, pred[8,33]{0,1:T(8,128)(4,1)} %constant.49), kind=kOutput, calls=%fused_computation.10 | convolution fusion | flops 313903104 | bytes 1255176 | tf_op jit(solution)/shard_map/conv_general_dilated | solution.py:22
  118.4 0.9 copy-done.1
  125.9 2.2 copy.115
  128.0 126.1 %all-reduce.3.cloned.1.call-done = (f32[64,64,3,3]{1,0,3,2:T(8,128)}, f32[64,64,3,3]{1,0,3,2:T(8,128)}) async-done(((f32[64,64,3,3]{1,0,3,2:T(8,128)}, f32[64,64,3,3]{1,0,3,2:T(8,128)}), (f32[64,64,3,3]{1,0,3,2:T(8,128)}, f32[64,64,3,3]{1,0,3,2:T(8,128)})) %all-reduce.3.cloned.1.call-update) | async-done | bytes 294928 | tf_op jit(solution)/shard_map/psum | solution.py:94
  254.1 1.7 broadcast_multiply_fusion
  255.8 1.7 broadcast_multiply_fusion.1
  (86 shorter events, 10.3 us)
Async XLA Ops:
  7.2 45.3 %copy-start = (bf16[64,64,3,3]{1,0,3,2:T(8,128)(2,1)S(1)}, bf16[64,64,3,3]{1,0,3,2:T(8,128)(2,1)}, u32[]{:S(2)}) copy-start(bf16[64,64,3,3]{1,0,3,2:T(8,128)(2,1)} %param.5) | copy-start | bytes 221188
  7.2 246.9 %all-reduce.3.cloned.1.call-start = ((), (), s32[]{:S(2)}) async-start(), calls=%async_computation | async-start | bytes 1179648 | tf_op jit(solution)/shard_map/psum | solution.py:94
  9.7 7.6 %collective-permute-start = (bf16[1,128,2,256]{3,1,2,0:T(8,128)(2,1)S(1)}, bf16[1,128,2,256]{3,1,2,0:T(8,128)(2,1)S(1)}, u32[]{:S(2)}, u32[]{:S(2)}) collective-permute-start(bf16[1,128,2,256]{3,1,2,0:T(8,128)(2,1)S(1)} %get-tuple-element.22), channel_id=1, source_target_pairs={{0,4},{1,5},{2,6},{3,7},{8,12},{9,13},{10,14},{11,15},{16,20},{17,... | collective-permute-start | bytes 393224 | tf_op jit(solution)/shard_map/ppermute | solution.py:15
  14.6 6.9 %collective-permute-start.1 = (bf16[1,128,2,256]{3,1,2,0:T(8,128)(2,1)S(1)}, bf16[1,128,2,256]{3,1,2,0:T(8,128)(2,1)S(1)}, u32[]{:S(2)}, u32[]{:S(2)}) collective-permute-start(bf16[1,128,2,256]{3,1,2,0:T(8,128)(2,1)S(1)} %get-tuple-element.23), channel_id=1, source_target_pairs={{4,0},{5,1},{6,2},{7,3},{12,8},{13,9},{14,10},{15,11},{20,16},{21,... | collective-permute-start | bytes 393224 | tf_op jit(solution)/shard_map/ppermute | solution.py:16
  17.3 14.7 %copy-start.9 = (bf16[1,128,2,256]{3,1,2,0:T(8,128)(2,1)}, bf16[1,128,2,256]{3,1,2,0:T(8,128)(2,1)S(1)}, u32[]{:S(2)}) copy-start(bf16[1,128,2,256]{3,1,2,0:T(8,128)(2,1)S(1)} %collective-permute-done) | copy-start | bytes 393220
  21.4 10.5 %copy-start.11 = (bf16[1,128,2,256]{3,1,2,0:T(8,128)(2,1)}, bf16[1,128,2,256]{3,1,2,0:T(8,128)(2,1)S(1)}, u32[]{:S(2)}) copy-start(bf16[1,128,2,256]{3,1,2,0:T(8,128)(2,1)S(1)} %collective-permute-done.1) | copy-start | bytes 393220
  22.2 5.1 %collective-permute-start.2 = (bf16[1,128,20,2]{1,3,2,0:T(2,128)(2,1)S(1)}, bf16[1,128,20,2]{1,3,2,0:T(2,128)(2,1)S(1)}, u32[]{:S(2)}, u32[]{:S(2)}) collective-permute-start(bf16[1,128,20,2]{1,3,2,0:T(2,128)(2,1)S(1)} %copy.72), channel_id=1, source_target_pairs={{0,1},{1,2},{2,3},{4,5},{5,6},{6,7},{8,9},{9,10},{10,11},{12,13},{... | collective-permute-start | bytes 30728 | tf_op jit(solution)/shard_map/ppermute | solution.py:15
  26.0 5.6 %collective-permute-start.3 = (bf16[1,128,20,2]{1,3,2,0:T(2,128)(2,1)S(1)}, bf16[1,128,20,2]{1,3,2,0:T(2,128)(2,1)S(1)}, u32[]{:S(2)}, u32[]{:S(2)}) collective-permute-start(bf16[1,128,20,2]{1,3,2,0:T(2,128)(2,1)S(1)} %copy.73), channel_id=1, source_target_pairs={{1,0},{2,1},{3,2},{5,4},{6,5},{7,6},{9,8},{10,9},{11,10},{13,12},{... | collective-permute-start | bytes 30728 | tf_op jit(solution)/shard_map/ppermute | solution.py:16
  27.8 6.3 %copy-start.3 = (bf16[1,128,20,2]{3,1,2,0:T(8,128)(2,1)}, bf16[1,128,20,2]{3,1,2,0:T(8,128)(2,1)S(1)}, u32[]{:S(2)}) copy-start(bf16[1,128,20,2]{3,1,2,0:T(8,128)(2,1)S(1)} %copy.74) | copy-start | bytes 30724
  32.0 0.9 copy-start.5
  46.8 5.7 %copy-start.7 = (bf16[64,20,1,8,33]{0,3,4,1,2:T(8,128)(2,1)S(1)}, bf16[64,20,1,8,33]{0,3,4,1,2:T(8,128)(2,1)}, u32[]{:S(2)}) copy-start(bf16[64,20,1,8,33]{0,3,4,1,2:T(8,128)(2,1)} %copy.78) | copy-start | bytes 2027524
  46.8 5.7 %copy-start.25 = (pred[8,33]{0,1:T(8,128)(4,1)S(1)}, pred[8,33]{0,1:T(8,128)(4,1)}, u32[]{:S(2)}) copy-start(pred[8,33]{0,1:T(8,128)(4,1)} %constant.50) | copy-start | bytes 796
  52.5 4.5 %copy-start.8 = (bf16[64,20,1,8,33]{0,3,4,1,2:T(8,128)(2,1)S(1)}, bf16[64,20,1,8,33]{0,3,4,1,2:T(8,128)(2,1)}, u32[]{:S(2)}) copy-start(bf16[64,20,1,8,33]{0,3,4,1,2:T(8,128)(2,1)} %copy.87) | copy-start | bytes 2027524
  52.5 4.5 %copy-start.24 = (bf16[64,64,3,3]{1,0,3,2:T(8,128)(2,1)S(1)}, bf16[64,64,3,3]{1,0,3,2:T(8,128)(2,1)}, u32[]{:S(2)}) copy-start(bf16[64,64,3,3]{1,0,3,2:T(8,128)(2,1)} %param.6) | copy-start | bytes 221188
  79.9 3.4 %copy-start.13 = (bf16[1,64,16,256]{3,2,1,0:T(8,128)(2,1)S(1)}, bf16[1,64,16,256]{3,2,1,0:T(8,128)(2,1)}, u32[]{:S(2)}) copy-start(bf16[1,64,16,256]{3,2,1,0:T(8,128)(2,1)} %param.7) | copy-start | bytes 1572868
  103.6 2.4 copy-start.2
  114.1 4.3 %copy-start.14 = (bf16[1,64,16,256]{3,2,1,0:T(8,128)(2,1)S(1)}, bf16[1,64,16,256]{3,2,1,0:T(8,128)(2,1)}, u32[]{:S(2)}) copy-start(bf16[1,64,16,256]{3,2,1,0:T(8,128)(2,1)} %param.4) | copy-start | bytes 1572868
  118.2 1.2 copy-start.1
  118.2 1.6 copy-start.21
  118.2 1.6 copy-start.22
  118.2 1.6 copy-start.23
  118.2 1.6 copy-start.15
  118.2 1.6 copy-start.16
  118.2 1.6 copy-start.17
  118.2 1.6 copy-start.18
  118.2 1.6 copy-start.19
  118.2 1.6 copy-start.20
  118.3 2.4 copy-start.6
  118.3 2.4 copy-start.10
  118.3 2.4 copy-start.12
  119.8 1.5 copy-start.4
Sparse Core Ops, SparseCore 0:
  125.8 128.2 all-reduce.2
where the time goes:
time: 265 us; the launch traced here: 264 us
  waiting for transfers between devices  135 us (51%)
  local copies, waits for them, and re-layouts  64.7 us (24%)
  matrix products  28.8 us (11%)
  between operations  14.6 us (6%)
  starting transfers between devices  11 us (4%)
  other arithmetic  9.86 us (4%)
    psum x1, waiting for transfers between devices, on_device(): lax.psum((first_grad, second_grad), ('dp', 'row', 'col'))  126 us
    conv_general_dilated x12, local copies, waits for them, and re-layouts, convolve(): lax.conv_general_dilated(padded, kernel, (1, 1), 'VALID', dimension_numbe...  32.1 us
    conv_general_dilated x4, matrix products, convolve(): lax.conv_general_dilated(padded, kernel, (1, 1), 'VALID', dimension_numbe...  15.2 us
    dot_general x18, matrix products, kernel_grad(): jnp.einsum('nihw,nohw->oi', window, upstream, preferred_element_type=jnp....  13.6 us
    mul x2, local copies, waits for them, and re-layouts, on_device(): act_padded = (jax.nn.silu(hidden) * inside).astype(jnp.bfloat16)  10.1 us
    mul x2, local copies, waits for them, and re-layouts, on_device(): hid_padded = (act_grad * silu_grad(hidden) * inside).astype(jnp.bfloat16)  9 us
    ppermute x2, starting transfers between devices, extended(): before = lax.ppermute(last, axis, up)  8.36 us
    ppermute x2, waiting for transfers between devices, extended(): after = lax.ppermute(leading, axis, down)  7.89 us
  transfers between devices with their start and end apart: 5, of which 4 were waited for; matrix products, arithmetic and copies ran while one was open for 1% of the time, Pallas kernels for 0%

commit v1 on v0

--- a/solution.py
+++ b/solution.py
@@ -3,6 +3,11 @@
 import jax.numpy as jnp
 from jax import lax
 from jax.sharding import PartitionSpec as P
+
+
+def samples_all_hold(a0):
+    clean = lax.psum(a0, ("row", "col"))
+    return lax.psum(clean, "dp")
 
 
 def extended(array, sides, width):
@@ -91,7 +96,7 @@
     hid_grad = hid_padded[:, :, 1:-1, 1:-1]
     input_grad = convolve(hid_padded, flipped(first_kernel)).astype(jnp.bfloat16)
     first_grad = kernel_grad(padded_in, hid_grad)
-    first_grad, second_grad = lax.psum((first_grad, second_grad), ("dp", "row", "col"))
+    first_grad, second_grad = samples_all_hold((first_grad, second_grad))
     return (outputs, input_grad, first_grad * factor, second_grad * factor)
 
 

time: 265 us -> 243 us (0.917)
  waiting for transfers between devices: 135 us -> 112 us
    psum x1 -> x2, waiting for transfers between devices: 126 us -> 103 us  [the longest x1 69.8 us: samples_all_hold(): clean = lax.psum(a0, ('row', 'col'))]
    unnamed x55 -> x41, local copies, waits for them, and re-layouts: 7.4 us -> 6.55 us
  transfers between devices with their start and end apart: 5 -> 6, of which waited for: 4 -> 5; matrix products, arithmetic and copies ran while one was open for 1% -> 2% of each run, Pallas kernels for 0% -> 0%
where the time goes in v1:
time: 243 us; the launch traced here: 242 us
  waiting for transfers between devices  112 us (46%)
  local copies, waits for them, and re-layouts  64 us (26%)
  matrix products  28.8 us (12%)
  between operations  14.5 us (6%)
  other arithmetic  11.6 us (5%)
  starting transfers between devices  11 us (5%)
    psum x1, waiting for transfers between devices, samples_all_hold(): clean = lax.psum(a0, ('row', 'col'))  69.8 us
    psum x1, waiting for transfers between devices, samples_all_hold(): return lax.psum(clean, 'dp')  33 us
    conv_general_dilated x12, local copies, waits for them, and re-layouts, convolve(): lax.conv_general_dilated(padded, kernel, (1, 1), 'VALID', dimension_numbe...  32.3 us
    dot_general x18, matrix products, kernel_grad(): jnp.einsum('nihw,nohw->oi', window, upstream, preferred_element_type=jnp....  15 us
    conv_general_dilated x4, matrix products, convolve(): lax.conv_general_dilated(padded, kernel, (1, 1), 'VALID', dimension_numbe...  13.8 us
    mul x2, local copies, waits for them, and re-layouts, on_device(): act_padded = (jax.nn.silu(hidden) * inside).astype(jnp.bfloat16)  10.1 us
    mul x2, local copies, waits for them, and re-layouts, on_device(): hid_padded = (act_grad * silu_grad(hidden) * inside).astype(jnp.bfloat16)  9.01 us
    ppermute x2, starting transfers between devices, extended(): before = lax.ppermute(last, axis, up)  8.36 us
  transfers between devices with their start and end apart: 6, of which 5 were waited for; matrix products, arithmetic and copies ran while one was open for 2% of the time, Pallas kernels for 0%

profile of v1, /device:TPU:0, one launch (start us, length us, event | category | flops | bytes accessed | tf_op | source)
XLA Modules:
  0.0 242.0 jit_solution(17789860501502150041)
XLA Ops:
  7.2 1.2 copy_dynamic-update-slice_fusion.1
  8.5 1.2 copy_dynamic-update-slice_fusion
  9.7 4.9 %collective-permute-start = (bf16[1,128,2,256]{3,1,2,0:T(8,128)(2,1)S(1)}, bf16[1,128,2,256]{3,1,2,0:T(8,128)(2,1)S(1)}, u32[]{:S(2)}, u32[]{:S(2)}) collective-permute-start(bf16[1,128,2,256]{3,1,2,0:T(8,128)(2,1)S(1)} %get-tuple-element.24), channel_id=1, source_target_pairs={{0,4},{1,5},{2,6},{3,7},{8,12},{9,13},{10,14},{11,15},{16,20},{17,... | collective-permute-start | bytes 393224 | tf_op jit(solution)/shard_map/ppermute | solution.py:20
  14.6 1.3 collective-permute-start.1
  15.9 1.4 collective-permute-done
  17.3 4.1 %collective-permute-done.1 = bf16[1,128,2,256]{3,1,2,0:T(8,128)(2,1)S(1)} collective-permute-done((bf16[1,128,2,256]{3,1,2,0:T(8,128)(2,1)S(1)}, bf16[1,128,2,256]{3,1,2,0:T(8,128)(2,1)S(1)}, u32[]{:S(2)}, u32[]{:S(2)}) %collective-permute-start.1) | collective-permute-done | bytes 131104 | tf_op jit(solution)/shard_map/ppermute | solution.py:21
  22.2 3.5 %collective-permute-start.2 = (bf16[1,128,20,2]{1,3,2,0:T(2,128)(2,1)S(1)}, bf16[1,128,20,2]{1,3,2,0:T(2,128)(2,1)S(1)}, u32[]{:S(2)}, u32[]{:S(2)}) collective-permute-start(bf16[1,128,20,2]{1,3,2,0:T(2,128)(2,1)S(1)} %copy.72), channel_id=1, source_target_pairs={{0,1},{1,2},{2,3},{4,5},{5,6},{6,7},{8,9},{9,10},{10,11},{12,13},{... | collective-permute-start | bytes 30728 | tf_op jit(solution)/shard_map/ppermute | solution.py:20
  26.0 1.3 collective-permute-start.3
  27.8 3.8 %collective-permute-done.3 = bf16[1,128,20,2]{1,3,2,0:T(2,128)(2,1)S(1)} collective-permute-done((bf16[1,128,20,2]{1,3,2,0:T(2,128)(2,1)S(1)}, bf16[1,128,20,2]{1,3,2,0:T(2,128)(2,1)S(1)}, u32[]{:S(2)}, u32[]{:S(2)}) %collective-permute-start.3) | collective-permute-done | bytes 10272 | tf_op jit(solution)/shard_map/ppermute | solution.py:21
  32.9 1.2 pad_maximum_fusion
  34.5 3.5 %reshape.214 = bf16[64,20,1,8,33]{4,3,0,1,2:T(8,128)(2,1)} reshape(bf16[64,20,1,264]{3,0,1,2:T(8,128)(2,1)S(1)} %pad) | data formatting | bytes 1351680 | tf_op jit(solution)/shard_map/conv_general_dilated | solution.py:27
  37.9 4.6 %copy.78 = bf16[64,20,1,8,33]{0,3,4,1,2:T(8,128)(2,1)} copy(bf16[64,20,1,8,33]{4,3,0,1,2:T(8,128)(2,1)} %reshape.214) | data formatting | bytes 1351680 | tf_op jit(solution)/shard_map/conv_general_dilated | solution.py:27
  42.6 0.9 slice.133
  43.6 3.3 %reshape.216 = bf16[64,20,1,8,33]{4,3,0,1,2:T(8,128)(2,1)} reshape(bf16[64,20,1,264]{3,0,1,2:T(8,128)(2,1)S(1)} %pad.4) | data formatting | bytes 1351680 | tf_op jit(solution)/shard_map/conv_general_dilated | solution.py:27
  46.9 4.7 %copy.87 = bf16[64,20,1,8,33]{0,3,4,1,2:T(8,128)(2,1)} copy(bf16[64,20,1,8,33]{4,3,0,1,2:T(8,128)(2,1)} %reshape.216) | data formatting | bytes 1351680 | tf_op jit(solution)/shard_map/conv_general_dilated | solution.py:27
  51.6 0.9 slice.138
  52.6 4.5 %fusion.4 = (f32[18,8,33,64]{3,1,2,0:T(8,128)}, f32[18,8,33,64]{3,1,2,0:T(8,128)S(1)}) fusion(pred[8,33]{0,1:T(8,128)(4,1)S(1)} %copy-done.18, bf16[64,64,3,3]{1,0,3,2:T(8,128)(2,1)S(1)} %copy-done, bf16[64,20,1,7,2]{0,3,4,1,2:T(8,128)(2,1)S(1)} %slice.133, bf16[64,20,1,8,33]{0,3,4,1,2:T(8,128)(2,1)S(1)} %copy-done.7), kind=kOutput, calls=%fused_computation.8 | convolution fusion | flops 354026496 | bytes 3218696 | tf_op jit(solution)/shard_map/conv_general_dilated | solution.py:27
  57.0 3.8 %select_multiply_fusion = f32[18,8,33,64]{3,1,2,0:T(8,128)} fusion(f32[18,8,33,64]{3,1,2,0:T(8,128)S(1)} %get-tuple-element.29, bf16[64,64,3,3]{1,0,3,2:T(8,128)(2,1)S(1)} %copy-done.15, bf16[64,20,1,7,2]{0,3,4,1,2:T(8,128)(2,1)S(1)} %slice.138, bf16[64,20,1,8,33]{0,3,4,1,2:T(8,128)(2,1)S(1)} %copy-done.8, pred[8,33]{0,1:T(8,128)(4,1)S(1)} %copy-done.18), kind=kOutput, calls=%fused_computation.6 | convolution fusion | flops 355547136 | bytes 3218696 | tf_op jit(solution)/shard_map/conv_general_dilated | solution.py:27
  60.8 5.2 %copy.127 = f32[18,8,33,64]{2,1,3,0:T(8,128)} copy(f32[18,8,33,64]{3,1,2,0:T(8,128)} %select_multiply_fusion) | data formatting | bytes 2433024 | tf_op jit(solution)/shard_map/mul | solution.py:95
  66.0 3.9 %reshape.213 = f32[18,1,264,64]{2,3,0,1:T(8,128)S(1)} reshape(f32[18,8,33,64]{2,1,3,0:T(8,128)} %copy.127) | data formatting | bytes 2433024 | tf_op jit(solution)/shard_map/mul | solution.py:95
  69.8 5.1 %copy.126 = f32[18,8,33,64]{2,1,3,0:T(8,128)} copy(f32[18,8,33,64]{3,1,2,0:T(8,128)} %get-tuple-element.28) | data formatting | bytes 2433024 | tf_op jit(solution)/shard_map/jit(silu)/mul | solution.py:90
  74.9 5.0 %reshape.212 = f32[18,1,264,64]{2,3,0,1:T(8,128)} reshape(f32[18,8,33,64]{2,1,3,0:T(8,128)} %copy.126) | data formatting | bytes 2433024 | tf_op jit(solution)/shard_map/jit(silu)/mul | solution.py:90
  79.9 3.5 %fusion.83 = (bf16[1,64,18,258]{3,1,2,0:T(8,128)(2,1)S(1)}, bf16[64,18,1,258]{3,0,1,2:T(8,128)(2,1)}, bf16[64,18,1,258]{3,0,1,2:T(8,128)(2,1)S(1)}, bf16[1,64,18,258]{3,1,2,0:T(8,128)(2,1)}) fusion(f32[18,258]{1,0:T(8,128)S(1)} %and_convert_fusion, f32[18,1,264,64]{2,3,0,1:T(8,128)} %reshape.212, f32[18,1,264,64]{2,3,0,1:T(8,128)S(1)} %reshape.213), kind=kLoop, calls=%fused_computation.124 | loop fusion | flops 1188864 | bytes 4774032 | tf_op jit(solution)/shard_map/convert_element_type | solution.py:90
  83.4 1.0 convolution_bitcast_fusion.3
  84.4 1.0 convolution_bitcast_fusion.4
  85.5 0.9 convolution_bitcast_fusion.5
  86.4 1.0 convolution_bitcast_fusion.6
  87.4 1.0 convolution_bitcast_fusion.7
  88.5 1.0 convolution_bitcast_fusion.8
  89.4 1.0 convolution_bitcast_fusion
  90.5 1.0 convolution_bitcast_fusion.1
  91.5 0.9 convolution_bitcast_fusion.2
  92.5 1.0 pad.6
  93.5 3.5 %reshape.217 = bf16[64,18,1,8,33]{4,3,0,1,2:T(8,128)(2,1)S(1)} reshape(bf16[64,18,1,264]{3,0,1,2:T(8,128)(2,1)} %pad.6) | data formatting | bytes 1216512 | tf_op jit(solution)/shard_map/conv_general_dilated | solution.py:27
  97.0 2.7 %copy.92 = bf16[64,18,1,8,33]{0,3,4,1,2:T(8,128)(2,1)} copy(bf16[64,18,1,8,33]{4,3,0,1,2:T(8,128)(2,1)S(1)} %reshape.217) | data formatting | bytes 1216512 | tf_op jit(solution)/shard_map/conv_general_dilated | solution.py:27
  100.6 2.9 %select_convert_fusion = bf16[16,8,33,64]{3,1,2,0:T(8,128)(2,1)S(1)} fusion(bf16[64,64,3,3]{1,0,3,2:T(8,128)(2,1)S(1)} %copy-done, bf16[64,18,1,7,2]{0,3,4,1,2:T(8,128)(2,1)S(1)} %slice.140, bf16[64,18,1,8,33]{0,3,4,1,2:T(8,128)(2,1)} %copy.92, pred[8,33]{0,1:T(8,128)(4,1)} %constant.49), kind=kOutput, calls=%fused_computation.9 | convolution fusion | flops 313903104 | bytes 1255176 | tf_op jit(solution)/shard_map/conv_general_dilated | solution.py:27
  103.9 2.2 copy.116
  106.0 1.0 pad.2
  107.1 3.5 %reshape.215 = bf16[64,18,1,8,33]{4,3,0,1,2:T(8,128)(2,1)S(1)} reshape(bf16[64,18,1,264]{3,0,1,2:T(8,128)(2,1)} %pad.2) | data formatting | bytes 1216512 | tf_op jit(solution)/shard_map/conv_general_dilated | solution.py:27
  110.6 2.7 %copy.83 = bf16[64,18,1,8,33]{0,3,4,1,2:T(8,128)(2,1)} copy(bf16[64,18,1,8,33]{4,3,0,1,2:T(8,128)(2,1)S(1)} %reshape.215) | data formatting | bytes 1216512 | tf_op jit(solution)/shard_map/conv_general_dilated | solution.py:27
  113.3 1.0 slice.135
  114.4 1.7 fusion.80
  123.7 2.7 %select_convert_fusion.1 = bf16[16,8,33,64]{3,1,2,0:T(8,128)(2,1)S(1)} fusion(bf16[64,64,3,3]{1,0,3,2:T(8,128)(2,1)S(1)} %copy-done.16, bf16[64,18,1,7,2]{0,3,4,1,2:T(8,128)(2,1)S(1)} %slice.135, bf16[64,18,1,8,33]{0,3,4,1,2:T(8,128)(2,1)S(1)} %copy-done.9, pred[8,33]{0,1:T(8,128)(4,1)S(1)} %copy-done.17), kind=kOutput, calls=%fused_computation.10 | convolution fusion | flops 313903104 | bytes 1255176 | tf_op jit(solution)/shard_map/conv_general_dilated | solution.py:27
  126.6 69.8 %all-reduce.5.cloned.1.call-done = (f32[64,64,3,3]{1,0,3,2:T(8,128)}, f32[64,64,3,3]{1,0,3,2:T(8,128)}) async-done(((f32[64,64,3,3]{1,0,3,2:T(8,128)}, f32[64,64,3,3]{1,0,3,2:T(8,128)}), (f32[64,64,3,3]{1,0,3,2:T(8,128)}, f32[64,64,3,3]{1,0,3,2:T(8,128)})) %all-reduce.5.cloned.1.call-update) | async-done | bytes 294928 | tf_op jit(solution)/shard_map/psum | solution.py:9
  196.6 2.2 copy.115
  198.7 33.0 %all-reduce.7.cloned.1.call-done = (f32[64,64,3,3]{1,0,3,2:T(8,128)}, f32[64,64,3,3]{1,0,3,2:T(8,128)}) async-done(((f32[64,64,3,3]{1,0,3,2:T(8,128)}, f32[64,64,3,3]{1,0,3,2:T(8,128)}), (f32[64,64,3,3]{1,0,3,2:T(8,128)}, f32[64,64,3,3]{1,0,3,2:T(8,128)})) %all-reduce.7.cloned.1.call-update) | async-done | bytes 294928 | tf_op jit(solution)/shard_map/psum | solution.py:10
  231.7 1.7 broadcast_multiply_fusion
  233.4 1.7 broadcast_multiply_fusion.1
  (75 shorter events, 12.5 us)
Async XLA Ops:
  7.2 45.4 %copy-start = (bf16[64,64,3,3]{1,0,3,2:T(8,128)(2,1)S(1)}, bf16[64,64,3,3]{1,0,3,2:T(8,128)(2,1)}, u32[]{:S(2)}) copy-start(bf16[64,64,3,3]{1,0,3,2:T(8,128)(2,1)} %param.5) | copy-start | bytes 221188
  7.2 189.2 %all-reduce.5.cloned.1.call-start = ((), (), s32[]{:S(2)}) async-start(), calls=%async_computation | async-start | bytes 1179648 | tf_op jit(solution)/shard_map/psum | solution.py:9
  9.7 7.6 %collective-permute-start = (bf16[1,128,2,256]{3,1,2,0:T(8,128)(2,1)S(1)}, bf16[1,128,2,256]{3,1,2,0:T(8,128)(2,1)S(1)}, u32[]{:S(2)}, u32[]{:S(2)}) collective-permute-start(bf16[1,128,2,256]{3,1,2,0:T(8,128)(2,1)S(1)} %get-tuple-element.24), channel_id=1, source_target_pairs={{0,4},{1,5},{2,6},{3,7},{8,12},{9,13},{10,14},{11,15},{16,20},{17,... | collective-permute-start | bytes 393224 | tf_op jit(solution)/shard_map/ppermute | solution.py:20
  14.6 6.9 %collective-permute-start.1 = (bf16[1,128,2,256]{3,1,2,0:T(8,128)(2,1)S(1)}, bf16[1,128,2,256]{3,1,2,0:T(8,128)(2,1)S(1)}, u32[]{:S(2)}, u32[]{:S(2)}) collective-permute-start(bf16[1,128,2,256]{3,1,2,0:T(8,128)(2,1)S(1)} %get-tuple-element.25), channel_id=1, source_target_pairs={{4,0},{5,1},{6,2},{7,3},{12,8},{13,9},{14,10},{15,11},{20,16},{21,... | collective-permute-start | bytes 393224 | tf_op jit(solution)/shard_map/ppermute | solution.py:21
  17.3 14.7 %copy-start.10 = (bf16[1,128,2,256]{3,1,2,0:T(8,128)(2,1)}, bf16[1,128,2,256]{3,1,2,0:T(8,128)(2,1)S(1)}, u32[]{:S(2)}) copy-start(bf16[1,128,2,256]{3,1,2,0:T(8,128)(2,1)S(1)} %collective-permute-done) | copy-start | bytes 393220
  21.4 10.5 %copy-start.12 = (bf16[1,128,2,256]{3,1,2,0:T(8,128)(2,1)}, bf16[1,128,2,256]{3,1,2,0:T(8,128)(2,1)S(1)}, u32[]{:S(2)}) copy-start(bf16[1,128,2,256]{3,1,2,0:T(8,128)(2,1)S(1)} %collective-permute-done.1) | copy-start | bytes 393220
  22.2 5.1 %collective-permute-start.2 = (bf16[1,128,20,2]{1,3,2,0:T(2,128)(2,1)S(1)}, bf16[1,128,20,2]{1,3,2,0:T(2,128)(2,1)S(1)}, u32[]{:S(2)}, u32[]{:S(2)}) collective-permute-start(bf16[1,128,20,2]{1,3,2,0:T(2,128)(2,1)S(1)} %copy.72), channel_id=1, source_target_pairs={{0,1},{1,2},{2,3},{4,5},{5,6},{6,7},{8,9},{9,10},{10,11},{12,13},{... | collective-permute-start | bytes 30728 | tf_op jit(solution)/shard_map/ppermute | solution.py:20
  26.0 5.6 %collective-permute-start.3 = (bf16[1,128,20,2]{1,3,2,0:T(2,128)(2,1)S(1)}, bf16[1,128,20,2]{1,3,2,0:T(2,128)(2,1)S(1)}, u32[]{:S(2)}, u32[]{:S(2)}) collective-permute-start(bf16[1,128,20,2]{1,3,2,0:T(2,128)(2,1)S(1)} %copy.73), channel_id=1, source_target_pairs={{1,0},{2,1},{3,2},{5,4},{6,5},{7,6},{9,8},{10,9},{11,10},{13,12},{... | collective-permute-start | bytes 30728 | tf_op jit(solution)/shard_map/ppermute | solution.py:21
  27.8 6.3 %copy-start.3 = (bf16[1,128,20,2]{3,1,2,0:T(8,128)(2,1)}, bf16[1,128,20,2]{3,1,2,0:T(8,128)(2,1)S(1)}, u32[]{:S(2)}) copy-start(bf16[1,128,20,2]{3,1,2,0:T(8,128)(2,1)S(1)} %copy.74) | copy-start | bytes 30724
  32.0 0.9 copy-start.5
  46.9 5.7 %copy-start.7 = (bf16[64,20,1,8,33]{0,3,4,1,2:T(8,128)(2,1)S(1)}, bf16[64,20,1,8,33]{0,3,4,1,2:T(8,128)(2,1)}, u32[]{:S(2)}) copy-start(bf16[64,20,1,8,33]{0,3,4,1,2:T(8,128)(2,1)} %copy.78) | copy-start | bytes 2027524
  46.9 5.7 %copy-start.18 = (pred[8,33]{0,1:T(8,128)(4,1)S(1)}, pred[8,33]{0,1:T(8,128)(4,1)}, u32[]{:S(2)}) copy-start(pred[8,33]{0,1:T(8,128)(4,1)} %constant.50) | copy-start | bytes 796
  52.5 4.5 %copy-start.8 = (bf16[64,20,1,8,33]{0,3,4,1,2:T(8,128)(2,1)S(1)}, bf16[64,20,1,8,33]{0,3,4,1,2:T(8,128)(2,1)}, u32[]{:S(2)}) copy-start(bf16[64,20,1,8,33]{0,3,4,1,2:T(8,128)(2,1)} %copy.87) | copy-start | bytes 2027524
  52.6 4.5 %copy-start.15 = (bf16[64,64,3,3]{1,0,3,2:T(8,128)(2,1)S(1)}, bf16[64,64,3,3]{1,0,3,2:T(8,128)(2,1)}, u32[]{:S(2)}) copy-start(bf16[64,64,3,3]{1,0,3,2:T(8,128)(2,1)} %param.6) | copy-start | bytes 221188
  79.9 3.5 %copy-start.14 = (bf16[1,64,16,256]{3,2,1,0:T(8,128)(2,1)S(1)}, bf16[1,64,16,256]{3,2,1,0:T(8,128)(2,1)}, u32[]{:S(2)}) copy-start(bf16[1,64,16,256]{3,2,1,0:T(8,128)(2,1)} %param.7) | copy-start | bytes 1572868
  103.7 2.4 copy-start.2
  113.3 5.3 %copy-start.1 = (bf16[1,64,18,258]{3,1,2,0:T(8,128)(2,1)S(1)}, bf16[1,64,18,258]{3,1,2,0:T(8,128)(2,1)}, u32[]{:S(2)}) copy-start(bf16[1,64,18,258]{3,1,2,0:T(8,128)(2,1)} %get-tuple-element.27) | copy-start | bytes 1783300
  113.3 5.3 %copy-start.6 = (bf16[1,128,20,2]{3,1,2,0:T(8,128)(2,1)S(1)}, bf16[1,128,20,2]{3,1,2,0:T(8,128)(2,1)}, u32[]{:S(2)}) copy-start(bf16[1,128,20,2]{3,1,2,0:T(8,128)(2,1)} %copy-done.5) | copy-start | bytes 30724
  113.3 5.3 %copy-start.11 = (bf16[1,128,2,256]{3,1,2,0:T(8,128)(2,1)S(1)}, bf16[1,128,2,256]{3,1,2,0:T(8,128)(2,1)}, u32[]{:S(2)}) copy-start(bf16[1,128,2,256]{3,1,2,0:T(8,128)(2,1)} %copy-done.10) | copy-start | bytes 393220
  113.3 5.3 %copy-start.13 = (bf16[1,128,2,256]{3,1,2,0:T(8,128)(2,1)S(1)}, bf16[1,128,2,256]{3,1,2,0:T(8,128)(2,1)}, u32[]{:S(2)}) copy-start(bf16[1,128,2,256]{3,1,2,0:T(8,128)(2,1)} %copy-done.12) | copy-start | bytes 393220
  116.1 3.1 %copy-start.4 = (bf16[1,128,20,2]{3,1,2,0:T(8,128)(2,1)S(1)}, bf16[1,128,20,2]{3,1,2,0:T(8,128)(2,1)}, u32[]{:S(2)}) copy-start(bf16[1,128,20,2]{3,1,2,0:T(8,128)(2,1)} %copy-done.3) | copy-start | bytes 30724
  122.4 1.3 copy-start.9
  122.5 1.3 copy-start.16
  122.5 1.3 copy-start.17
  123.6 108.1 %all-reduce.7.cloned.1.call-start = ((), (), s32[]{:S(2)}) async-start(), calls=%async_computation.1 | async-start | bytes 1179648 | tf_op jit(solution)/shard_map/psum | solution.py:10
Sparse Core Ops, SparseCore 0:
  123.7 72.5 all-reduce.4
  198.7 32.9 all-reduce.6
